TPU v7x, 256 devices: a 4x2x16 block of a 4x16x16 slice. The times are simulated.
256 devices in a mesh: slides: 2 (over y), row: 128 (over x, z, core).
Axes of the slice: x: 4, y: 2, z: 16, core: 2. Of those that a mesh axis runs over, the one named last changes fastest.
The devices are a block of a 4x16x16 slice.
Arguments:
- slide_pixels: bfloat16 [16384, 16384], P(('slides', 'row')), parts along dimension 0, may hold values from -6 to 6
- tissue_mask: int32 [512, 8], P(('slides', 'row')), parts along dimension 0, may hold values from 0 to 1, as said below
- conv_weight: bfloat16 [3, 3, 64, 64], replicated, may hold values from -0.25 to 0.25
- conv_bias: bfloat16 [64], replicated, may hold values from -3 to 3
Outputs:
- packed_tiles: bfloat16 [2048, 32, 2048], P(('slides', 'row')), parts along dimension 0
There are 2 independent parts, one for each index of `slides`. A program takes and returns all parts, laid end to end along the dimension named above; an argument that names none is the same for every part. Nothing has to cross between parts.
Inputs may be any that keep to these rules, and one draw needn't show every extreme that they name: `tissue_mask`: exactly 1024 tiles hold tissue. For every s from 1 to 127, the first s * 2 tile rows hold s * 8 + e tissue tiles with e between 0 and 2; e = 2 occurs in every draw. For every such s, some column holds tissue in both tile row s * 2 - 1 and tile row s * 2.
All inputs are finite; a program needn't handle non-finite values.
Results may differ from a plain program's by a relative error of at most 0.001.
Values may be sent and summed in bfloat16 or wider, within the bound.
No kernel may reach another device: no remote copies, remote signals or barrier semaphores. Data moves between devices by JAX's collectives and lax.ppermute only.
A program may use at most 64 MiB of HBM per device.

v0:
```python
import jax
import jax.numpy as jnp
from jax import lax
from jax.sharding import Mesh
from jax.sharding import PartitionSpec as P

SLOTS = 8
SHIFT_MOST = 2
ROW = ("row_0", "row_1", "row_2")
SLIDES_ROW = ("slides", "row_0", "row_1", "row_2")


def extended(array, sides, width):
    for axis, dim in sides:
        size, length = (lax.axis_size(axis), array.shape[dim])
        up = [(i, (i + 1) % size) for i in range(size - 1)]
        down = [(j, i) for i, j in up]
        last = lax.slice_in_dim(array, length - width, length, axis=dim)
        initial = lax.slice_in_dim(array, 0, width, axis=dim)
        before = lax.ppermute(last, axis, up)
        after = lax.ppermute(initial, axis, down)
        array = jnp.concatenate([before, array, after], axis=dim)
    return array


def in_order(pieces, dim):
    pieces = jnp.moveaxis(pieces, 0, dim)
    dims = pieces.shape
    return pieces.reshape(*dims[:dim], dims[dim] * dims[dim + 1], *dims[dim + 2 :])


def gather_in_order(array, axes, turns):
    pieces = array
    for k in turns:
        pieces = lax.all_gather(pieces, axes[k])
    done = turns[::-1]
    back = [done.index(k) for k in range(len(axes))]
    pieces = pieces.transpose(*back, *range(len(axes), pieces.ndim))
    return pieces.reshape(-1, *array.shape)


def whole_of(array, axes, turns, dim):
    return in_order(gather_in_order(array, axes, turns), dim)


def passed_along(array, axis, by):
    length = lax.axis_size(axis)
    pairs = [(i, i + by) for i in range(length) if 0 <= i + by < length]
    return lax.ppermute(array, axis, pairs)


def convolve(padded, conv_weight, conv_bias):
    tile_count = padded.shape[0]
    channels = conv_weight.shape[2]
    side = padded.shape[1] - 2
    pixels = padded.reshape(tile_count, side + 2, side + 2, channels)
    widened = jnp.concatenate(
        [pixels[:, :, 0:side], pixels[:, :, 1 : side + 1], pixels[:, :, 2 : side + 2]], axis=3
    )
    result = jnp.zeros((tile_count, side, side, channels), jnp.float32)
    for vertical in range(3):
        kernel = conv_weight[vertical].reshape(3 * channels, channels)
        result = result + jnp.einsum(
            "nhwk,ko->nhwo",
            widened[:, vertical : vertical + side],
            kernel,
            preferred_element_type=jnp.float32,
        )
    result = result + conv_bias.astype(jnp.float32)
    return result.astype(jnp.bfloat16).reshape(tile_count, side, side * channels)


def on_device(slide_pixels, tissue_mask, conv_weight, conv_bias):
    band_rows, grid_cols = tissue_mask.shape
    channels = conv_weight.shape[2]
    side = slide_pixels.shape[0] // band_rows
    tile_total = band_rows * grid_cols
    flat_mask = tissue_mask.reshape(tile_total)
    own_count = jnp.sum(flat_mask)
    blocks = slide_pixels.reshape(band_rows, side, grid_cols, side, channels)
    keeps = tissue_mask.astype(jnp.bfloat16)[:, None, :, None, None]
    masked = (blocks * keeps).reshape(band_rows * side, grid_cols * side * channels)
    haloed = extended(masked, ((ROW, 0),), 1)
    widened = haloed.reshape(band_rows * side + 2, grid_cols * side, channels)
    widened = jnp.pad(widened, ((0, 0), (1, 1), (0, 0)))
    pieces = []
    for tile_row in range(band_rows):
        for tile_col in range(grid_cols):
            window = widened[
                tile_row * side : tile_row * side + side + 2,
                tile_col * side : tile_col * side + side + 2,
            ]
            pieces.append(window.reshape(side + 2, (side + 2) * channels))
    padded_tiles = jnp.stack(pieces)
    device = lax.axis_index(ROW)
    table = whole_of(own_count.reshape(1), (("row_0", "row_1"), "row_2"), (0, 1), 0)
    lower = jnp.arange(table.shape[0], dtype=jnp.int32) < device
    earlier = jnp.sum(jnp.where(lower, table, jnp.zeros_like(table)))
    order = jnp.argsort(1 - flat_mask, stable=True)
    first_rank = device * SLOTS

    def select(start, amount):
        ranks = start + jnp.arange(amount, dtype=jnp.int32)
        local = ranks - earlier
        present = (local >= 0) & (local < own_count)
        where_tile = jnp.take(order, jnp.clip(local, 0, tile_total - 1), axis=0)
        chosen = jnp.take(padded_tiles, where_tile, axis=0)
        return (chosen, present)

    kept, kept_live = select(first_rank, SLOTS)
    onward, onward_live = select(first_rank + SLOTS, SHIFT_MOST)
    upper = SLOTS - SHIFT_MOST

    def keep_live(values, live):
        return jnp.where(live[:, None, None], values, jnp.zeros_like(values))

    from_prev = passed_along(keep_live(onward, onward_live), ROW, 1)
    owned = keep_live(kept, kept_live) + jnp.pad(from_prev, ((0, upper), (0, 0), (0, 0)))
    return convolve(owned, conv_weight, conv_bias)


def solution(mesh):
    finer = Mesh(
        mesh.devices.reshape(mesh.shape["slides"], 4, 16, 2), ("slides", "row_0", "row_1", "row_2")
    )
    return jax.shard_map(
        on_device,
        mesh=finer,
        in_specs=(P(SLIDES_ROW, None), P(SLIDES_ROW, None), P(), P()),
        out_specs=P(SLIDES_ROW, None, None),
        check_vma=False,
    )
```

profile of v0, /device:TPU:44, one launch (start us, length us, event | category | flops | bytes accessed | tf_op | source)
XLA Modules:
  0.0 155.1 jit_solution(15150391593055640642)
XLA Ops:
  0.0 1.4 fusion.19
  1.4 3.0 %mul.23 = bf16[2,32,8,32,64]{4,3,2,1,0:T(8,128)(2,1)} broadcast(bf16[2,8]{1,0:T(2,128)(2,1)S(1)} %get-tuple-element.34), dimensions={0,2} | broadcast | bytes 2097184 | tf_op jit(solution)/shard_map/mul | solution.py:82
  4.4 6.0 %mul.24 = bf16[64,16384]{1,0:T(8,128)(2,1)} reshape(bf16[2,32,8,32,64]{4,3,2,1,0:T(8,128)(2,1)} %mul.23) | data formatting | bytes 4194304 | tf_op jit(solution)/shard_map/mul | solution.py:82
  10.4 2.7 %mul.25 = bf16[64,16384]{1,0:T(8,128)(2,1)S(1)} multiply(bf16[64,16384]{1,0:T(8,128)(2,1)} %param.4, bf16[64,16384]{1,0:T(8,128)(2,1)} %mul.24) | non-fusion elementwise | flops 1048576 | bytes 6291456 | tf_op jit(solution)/shard_map/mul | solution.py:82
  13.2 2.0 %collective-permute-start = (bf16[1,16384]{1,0:T(2,128)(2,1)S(1)}, bf16[1,16384]{1,0:T(2,128)(2,1)S(1)}, u32[]{:S(2)}, u32[]{:S(2)}) collective-permute-start(bf16[1,16384]{1,0:T(2,128)(2,1)S(1)} %get-tuple-element.28), channel_id=1, source_target_pairs={{0,1},{1,2},{2,3},{3,4},{4,5},{5,6},{6,7},{7,8},{8,9},{9,10},{10,1... | collective-permute-start | bytes 98312 | tf_op jit(solution)/shard_map/ppermute | solution.py:20
  15.2 23.7 %collective-permute-start.1 = (bf16[1,16384]{1,0:T(2,128)(2,1)S(1)}, bf16[1,16384]{1,0:T(2,128)(2,1)S(1)}, u32[]{:S(2)}, u32[]{:S(2)}) collective-permute-start(bf16[1,16384]{1,0:T(2,128)(2,1)S(1)} %get-tuple-element.29), channel_id=1, source_target_pairs={{1,0},{2,1},{3,2},{4,3},{5,4},{6,5},{7,6},{8,7},{9,8},{10,9},{11,1... | collective-permute-start | bytes 98312 | tf_op jit(solution)/shard_map/ppermute | solution.py:21
  40.1 1.3 dynamic-update-slice
  41.4 23.8 %all-reduce.2 = s32[64]{0:T(128)S(1)} all-reduce(s32[64]{0:T(128)S(1)} %dynamic-update-slice), channel_id=1, replica_groups=mesh['slides'=2,'row_0'=4,'row_1'=16,'row_2'=2] {'row_0','row_1'}, use_global_device_ids=true, to_apply=%add.2 | all-reduce | flops 64 | bytes 512
  66.2 1.8 %all-reduce.3 = s32[128]{0:T(128)S(1)} all-reduce(s32[128]{0:T(128)S(1)} %dynamic-update-slice.1), channel_id=2, replica_groups=mesh['slides'=2,'row_0'=4,'row_1'=16,'row_2'=2] {'row_2'}, use_global_device_ids=true, to_apply=%add.3 | all-reduce | flops 128 | bytes 1024
  69.7 1.2 sort.17
  72.3 1.4 compare_and_fusion.2
  75.7 1.4 compare_and_fusion
  77.1 5.7 %concatenate.30 = bf16[64,256,64]{2,1,0:T(8,128)(2,1)} reshape(bf16[64,16384]{1,0:T(8,128)(2,1)S(1)} %mul.25) | data formatting | bytes 4194304 | tf_op jit(solution)/shard_map/concatenate | solution.py:22
  83.4 4.5 %constant_dynamic-update-slice_fusion.3 = (bf16[65,256,64]{2,1,0:T(8,128)(2,1)S(1)}, bf16[65,256,64]{2,1,0:T(8,128)(2,1)S(1)}) fusion(bf16[64,256,64]{2,1,0:T(8,128)(2,1)} %concatenate.30, bf16[65,256,64]{2,1,0:T(8,128)(2,1)S(1)} %constant_dynamic-update-slice_fusion.1), kind=kLoop, calls=%fused_computation.19 | loop fusion | bytes 10485760
  87.9 6.4 %fusion.5 = bf16[66,258,64]{2,1,0:T(8,128)(2,1)} fusion(bf16[1,256,64]{2,1,0:T(8,128)(2,1)S(1)} %concatenate.31, bf16[64,256,64]{2,1,0:T(8,128)(2,1)S(1)} %copy-done, bf16[1,256,64]{2,1,0:T(8,128)(2,1)S(1)} %concatenate.29), kind=kLoop, calls=%fused_computation.11 | loop fusion | flops 13077504 | bytes 4342272 | tf_op jit(solution)/shard_map/concatenate | solution.py:22
  94.4 1.0 fusion.14
  95.6 1.6 %fusion.13 = (bf16[34,34,64]{2,1,0:T(8,128)(2,1)S(1)}, bf16[34,34,64]{2,1,0:T(8,128)(2,1)S(1)}, bf16[34,34,64]{2,1,0:T(8,128)(2,1)S(1)}, bf16[34,34,64]{2,1,0:T(8,128)(2,1)S(1)}) fusion(bf16[66,258,64]{2,1,0:T(8,128)(2,1)} %fusion.5), kind=kLoop, calls=%fused_computation.67 | loop fusion | bytes 1183744 | tf_op jit(solution)/shard_map/slice | solution.py:89
  98.4 0.9 stack_reshape.55
  99.3 0.9 stack_reshape.48
  102.0 0.9 stack_reshape.59
  103.8 0.9 stack_reshape.57
  104.8 2.7 %fusion.15 = (bf16[34,34,64]{2,1,0:T(8,128)(2,1)S(1)}, bf16[34,34,64]{2,1,0:T(8,128)(2,1)S(1)}, bf16[34,34,64]{2,1,0:T(8,128)(2,1)S(1)}, bf16[34,34,64]{2,1,0:T(...) fusion(bf16[65,256,64]{2,1,0:T(8,128)(2,1)} %copy-done.2), kind=kLoop, calls=%fused_computation.69 | loop fusion | bytes 1775616 | tf_op jit(solution)/shard_map/slice | solution.py:89
  109.3 0.9 stack_reshape.52
  112.9 0.9 constant_dynamic-update-slice_fusion.19
  113.8 0.9 constant_dynamic-update-slice_fusion.18
  114.8 0.9 constant_dynamic-update-slice_fusion.17
  115.7 0.9 constant_dynamic-update-slice_fusion.16
  116.7 0.9 constant_dynamic-update-slice_fusion.15
  117.6 0.9 constant_dynamic-update-slice_fusion.14
  118.5 0.9 constant_dynamic-update-slice_fusion.13
  119.5 0.9 constant_dynamic-update-slice_fusion.12
  120.4 0.9 constant_dynamic-update-slice_fusion.11
  121.4 0.9 constant_dynamic-update-slice_fusion.10
  122.3 0.9 constant_dynamic-update-slice_fusion.9
  123.2 0.9 constant_dynamic-update-slice_fusion.8
  124.2 0.9 constant_dynamic-update-slice_fusion.7
  125.1 0.9 constant_dynamic-update-slice_fusion.6
  126.8 2.2 %collective-permute-start.2 = (bf16[2,34,2176]{2,1,0:T(8,128)(2,1)S(1)}, bf16[2,34,2176]{2,1,0:T(8,128)(2,1)}, u32[]{:S(2)}, u32[]{:S(2)}) collective-permute-start(bf16[2,34,2176]{2,1,0:T(8,128)(2,1)S(1)} %select_select_fusion), channel_id=1, source_target_pairs={{0,1},{1,2},{2,3},{3,4},{4,5},{5,6},{6,7},{7,8},{8,9},{9,10},{10,1... | collective-permute-start | bytes 887816 | tf_op jit(solution)/shard_map/ppermute | solution.py:49
  129.0 1.5 fusion.18
  130.5 2.5 %gather_fusion.1 = bf16[8,34,2176]{2,1,0:T(8,128)(2,1)S(1)} fusion(bf16[16,34,2176]{2,1,0:T(8,128)(2,1)} %copy-done.1, s32[1024]{0:T(1024)S(1)} %pad_clamp_fusion.2), kind=kCustom, calls=%fused_computation.1 | custom fusion | bytes 2367520 | tf_op jit(solution)/shard_map/jit(_take)/gather | solution.py:107
  133.1 4.6 %collective-permute-done.2 = bf16[2,34,2176]{2,1,0:T(8,128)(2,1)} collective-permute-done((bf16[2,34,2176]{2,1,0:T(8,128)(2,1)S(1)}, bf16[2,34,2176]{2,1,0:T(8,128)(2,1)}, u32[]{:S(2)}, u32[]{:S(2)}) %collective-permute-start.2) | collective-permute-done | bytes 295968 | tf_op jit(solution)/shard_map/ppermute | solution.py:49
  137.7 2.4 %pad_add_fusion = bf16[8,34,2176]{2,1,0:T(8,128)(2,1)} fusion(bf16[2,34,2176]{2,1,0:T(8,128)(2,1)} %collective-permute-done.2, bf16[8,34,2176]{2,1,0:T(8,128)(2,1)S(1)} %gather_fusion.1, pred[8]{0:T(512)(128)(4,1)S(1)} %get-tuple-element.38, pred[8]{0:T(512)(128)(4,1)S(1)} %get-tuple-element.39), kind=kLoop, calls=%fused_computation.14 | loop fusion | flops 1775616 | bytes 2663440 | tf_op jit(solution)/shard_map/add | solution.py:118
  140.1 3.3 %reshape.219 = bf16[8,34,34,64]{3,2,1,0:T(8,128)(2,1)S(1)} reshape(bf16[8,34,2176]{2,1,0:T(8,128)(2,1)} %pad_add_fusion) | data formatting | bytes 2367488 | tf_op jit(solution)/shard_map/reshape | solution.py:56
  143.4 1.6 %fusion.16 = (bf16[8,34,32,64]{3,2,1,0:T(8,128)(2,1)S(1)}, bf16[8,34,32,64]{3,2,1,0:T(8,128)(2,1)S(1)}, bf16[8,34,32,64]{3,2,1,0:T(8,128)(2,1)S(1)}) fusion(bf16[8,34,34,64]{3,2,1,0:T(8,128)(2,1)S(1)} %reshape.219), kind=kLoop, calls=%fused_computation.70 | loop fusion | bytes 6684672 | tf_op jit(solution)/shard_map/slice | solution.py:58
  145.1 2.4 %fusion.11 = f32[8,32,32,64]{3,2,1,0:T(8,128)S(1)} fusion(bf16[192,64,1,1]{1,0,3,2:T(8,128)(2,1)S(1)} %bitcast.39, bf16[8,34,32,64]{3,2,1,0:T(8,128)(2,1)S(1)} %get-tuple-element.27, bf16[8,34,32,64]{3,2,1,0:T(8,128)(2,1)S(1)} %get-tuple-element.26, bf16[8,34,32,64]{3,2,1,0:T(8,128)(2,1)S(1)} %get-tuple-element.25), kind=kOutput, calls=%fused_computation.65 | convolution fusion | flops 211353600 | bytes 5464064 | tf_op jit(solution)/shard_map/nhwk,ko->nhwo/dot_general | solution.py:63
  147.5 2.3 %fusion.12 = f32[8,32,32,64]{3,2,1,0:T(8,128)S(1)} fusion(bf16[192,64,1,1]{1,0,3,2:T(8,128)(2,1)S(1)} %bitcast.38, bf16[8,34,32,64]{3,2,1,0:T(8,128)(2,1)S(1)} %get-tuple-element.27, bf16[8,34,32,64]{3,2,1,0:T(8,128)(2,1)S(1)} %get-tuple-element.26, bf16[8,34,32,64]{3,2,1,0:T(8,128)(2,1)S(1)} %get-tuple-element.25), kind=kOutput, calls=%fused_computation.66 | convolution fusion | flops 211353600 | bytes 5464064 | tf_op jit(solution)/shard_map/nhwk,ko->nhwo/dot_general | solution.py:63
  149.8 2.8 %add_convert_fusion = bf16[8,32,32,64]{3,2,1,0:T(8,128)(2,1)S(1)} fusion(f32[8,32,32,64]{3,2,1,0:T(8,128)S(1)} %fusion.12, f32[8,32,32,64]{3,2,1,0:T(8,128)S(1)} %fusion.11, bf16[192,64,1,1]{1,0,3,2:T(8,128)(2,1)S(1)} %bitcast.37, f32[64]{0:T(128)S(1)} %convert_element_type.14, bf16[8,34,32,64]{3,2,1,0:T(8,128)(2,1)S(1)} %get-tuple-element.27, ...), kind=kOutput, calls=%fused_computation.13 | convolution fusion | flops 213450752 | bytes 8610048 | tf_op jit(solution)/shard_map/nhwk,ko->nhwo/dot_general | solution.py:63
  152.6 2.4 %reshape.169 = bf16[8,32,2048]{2,1,0:T(8,128)(2,1)} reshape(bf16[8,32,32,64]{3,2,1,0:T(8,128)(2,1)S(1)} %add_convert_fusion) | data formatting | bytes 2097152 | tf_op jit(solution)/shard_map/reshape | solution.py:70
  (60 shorter events, 16.6 us)
Async XLA Ops:
  10.4 28.5 %copy-start.7 = (u32[256]{0:T(256)S(1)}, u32[256]{0:T(256)}, u32[]{:S(2)}) copy-start(u32[256]{0:T(256)} %constant.98) | copy-start | bytes 3076
  10.4 29.2 %copy-start.6 = (u32[256]{0:T(256)S(1)}, u32[256]{0:T(256)}, u32[]{:S(2)}) copy-start(u32[256]{0:T(256)} %constant.93) | copy-start | bytes 3076
  13.2 69.6 %collective-permute-start = (bf16[1,16384]{1,0:T(2,128)(2,1)S(1)}, bf16[1,16384]{1,0:T(2,128)(2,1)S(1)}, u32[]{:S(2)}, u32[]{:S(2)}) collective-permute-start(bf16[1,16384]{1,0:T(2,128)(2,1)S(1)} %get-tuple-element.28), channel_id=1, source_target_pairs={{0,1},{1,2},{2,3},{3,4},{4,5},{5,6},{6,7},{7,8},{8,9},{9,10},{10,1... | collective-permute-start | bytes 98312 | tf_op jit(solution)/shard_map/ppermute | solution.py:20
  15.2 67.9 %collective-permute-start.1 = (bf16[1,16384]{1,0:T(2,128)(2,1)S(1)}, bf16[1,16384]{1,0:T(2,128)(2,1)S(1)}, u32[]{:S(2)}, u32[]{:S(2)}) collective-permute-start(bf16[1,16384]{1,0:T(2,128)(2,1)S(1)} %get-tuple-element.29), channel_id=1, source_target_pairs={{1,0},{2,1},{3,2},{4,3},{5,4},{6,5},{7,6},{8,7},{9,8},{10,9},{11,1... | collective-permute-start | bytes 98312 | tf_op jit(solution)/shard_map/ppermute | solution.py:21
  77.0 5.7 %copy-start.5 = (bf16[64]{0:T(256)(128)(2,1)S(1)}, bf16[64]{0:T(256)(128)(2,1)}, u32[]{:S(2)}) copy-start(bf16[64]{0:T(256)(128)(2,1)} %param.7) | copy-start | bytes 388
  83.4 4.5 %copy-start = (bf16[64,256,64]{2,1,0:T(8,128)(2,1)S(1)}, bf16[64,256,64]{2,1,0:T(8,128)(2,1)}, u32[]{:S(2)}) copy-start(bf16[64,256,64]{2,1,0:T(8,128)(2,1)} %concatenate.30) | copy-start | bytes 6291460
  87.9 6.5 %copy-start.2 = (bf16[65,256,64]{2,1,0:T(8,128)(2,1)}, bf16[65,256,64]{2,1,0:T(8,128)(2,1)S(1)}, u32[]{:S(2)}) copy-start(bf16[65,256,64]{2,1,0:T(8,128)(2,1)S(1)} %get-tuple-element.24) | copy-start | bytes 6389764
  126.1 2.9 %copy-start.1 = (bf16[16,34,2176]{2,1,0:T(8,128)(2,1)}, bf16[16,34,2176]{2,1,0:T(8,128)(2,1)S(1)}, u32[]{:S(2)}) copy-start(bf16[16,34,2176]{2,1,0:T(8,128)(2,1)S(1)} %constant_dynamic-update-slice_fusion.4) | copy-start | bytes 7102468
  126.8 10.9 %collective-permute-start.2 = (bf16[2,34,2176]{2,1,0:T(8,128)(2,1)S(1)}, bf16[2,34,2176]{2,1,0:T(8,128)(2,1)}, u32[]{:S(2)}, u32[]{:S(2)}) collective-permute-start(bf16[2,34,2176]{2,1,0:T(8,128)(2,1)S(1)} %select_select_fusion), channel_id=1, source_target_pairs={{0,1},{1,2},{2,3},{3,4},{4,5},{5,6},{6,7},{7,8},{8,9},{9,10},{10,1... | collective-permute-start | bytes 887816 | tf_op jit(solution)/shard_map/ppermute | solution.py:49
  143.4 1.6 %copy-start.4 = (bf16[1,3,64,64]{3,2,1,0:T(8,128)(2,1)S(1)}, bf16[1,3,64,64]{3,2,1,0:T(8,128)(2,1)}, u32[]{:S(2)}) copy-start(bf16[1,3,64,64]{3,2,1,0:T(8,128)(2,1)} %get-tuple-element.32) | copy-start | bytes 73732
  145.1 2.4 %copy-start.3 = (bf16[1,3,64,64]{3,2,1,0:T(8,128)(2,1)S(1)}, bf16[1,3,64,64]{3,2,1,0:T(8,128)(2,1)}, u32[]{:S(2)}) copy-start(bf16[1,3,64,64]{3,2,1,0:T(8,128)(2,1)} %get-tuple-element.31) | copy-start | bytes 73732
where the time goes:
time: 157 us; the launch traced here: 155 us
  local copies, waits for them, and re-layouts  67.5 us (43%)
  starting transfers between devices  27.8 us (18%)
  blocking collectives  25.7 us (16%)
  other arithmetic  20.9 us (13%)
  matrix products  7.52 us (5%)
  waiting for transfers between devices  4.62 us (3%)
    unnamed x2, blocking collectives  25.7 us
    ppermute x1, starting transfers between devices, extended(): after = lax.ppermute(initial, axis, down)  23.7 us
    unnamed x39, local copies, waits for them, and re-layouts  20.5 us
    another operation x17, local copies, waits for them, and re-layouts, on_device(): padded_tiles = jnp.stack(pieces)  13.3 us
    mul x2, local copies, waits for them, and re-layouts, on_device(): blocks * keeps  8.98 us
    dot_general x3, matrix products, convolve(): jnp.einsum('nhwk,ko->nhwo', widened[:, vertical:vertical + side], kernel,...  7.52 us
    concatenate x1, other arithmetic, extended(): array = jnp.concatenate([before, array, after], axis=dim)  6.45 us
    concatenate x4, local copies, waits for them, and re-layouts, extended(): array = jnp.concatenate([before, array, after], axis=dim)  5.9 us
  transfers between devices with their start and end apart: 3, of which 1 were waited for; matrix products, arithmetic and copies ran while one was open for 14% of the time, Pallas kernels for 0%

commit v1 on v0

v1 whole, which is shorter than its diff:
```python
import functools

import jax
import jax.numpy as jnp
from jax import lax
from jax.experimental import pallas as pl
from jax.experimental.pallas import tpu as pltpu
from jax.sharding import PartitionSpec as P

SLOTS = 8
SHIFT_MOST = 2
LANES = 128
GUARD = 16


def edge_kernel(mask, first_rows, last_rows, first, last, *, grid_cols, tile_lanes):
    for col in range(grid_cols):
        lanes = pl.ds(col * tile_lanes, tile_lanes)
        top = first_rows[0:1, lanes]
        first[:, lanes] = jnp.where(mask[0, col] == 1, top, jnp.zeros_like(top))
        low = last_rows[last_rows.shape[0] - 1 :, lanes]
        last[:, lanes] = jnp.where(mask[1, col] == 1, low, jnp.zeros_like(low))


def edges(mask, pixels):
    band, width = pixels.shape
    grid_cols = mask.shape[1]
    step = 16
    row = jax.ShapeDtypeStruct((1, width), pixels.dtype)
    whole = pl.BlockSpec((1, width), lambda i: (0, 0))
    return pl.pallas_call(
        functools.partial(edge_kernel, grid_cols=grid_cols, tile_lanes=width // grid_cols),
        grid=(1,),
        in_specs=[
            pl.BlockSpec(memory_space=pltpu.SMEM),
            pl.BlockSpec((step, width), lambda i: (0, 0)),
            pl.BlockSpec((step, width), lambda i: (band // step - 1, 0)),
        ],
        out_specs=[whole, whole],
        out_shape=[row, row],
    )(mask, pixels, pixels)


def conv_kernel(
    mask, pixels, above, below, weight, bias, tiles, tail,
    band, shifted, banded, made, in_sem, out_sem, tail_sem,
    *, rows, cols, side, ch,
):
    wide = side * ch
    count = rows * cols

    def tissue(t):
        return mask[t // cols, t % cols]

    def fetch(t):
        row, col = t // cols, t % cols
        return pltpu.make_async_copy(
            pixels.at[pl.ds(row * side, side), pl.ds(col * wide, wide)],
            band.at[pl.ds(GUARD + row * side, side), pl.ds(LANES + col * wide, wide)],
            in_sem.at[t],
        )

    for t in range(count):
        row, col = t // cols, t % cols

        @pl.when(tissue(t) == 1)
        def _():
            fetch(t).start()

        @pl.when(tissue(t) != 1)
        def _():
            band[GUARD + row * side : GUARD + (row + 1) * side, LANES + col * wide : LANES + (col + 1) * wide] = (
                jnp.zeros((side, wide), band.dtype)
            )

    edge = jnp.zeros((band.shape[0], LANES), band.dtype)
    band[:, 0:LANES] = edge
    band[:, LANES + cols * wide :] = edge
    inner = pl.ds(LANES, cols * wide)
    band[0:GUARD, inner] = jnp.broadcast_to(above[...], (GUARD, cols * wide))
    band[GUARD + rows * side :, inner] = jnp.broadcast_to(below[...], (GUARD, cols * wide))

    spread = lax.broadcasted_iota(jnp.int32, (ch, 2 * ch), 1) - lax.broadcasted_iota(jnp.int32, (ch, 2 * ch), 0)
    taps = weight[...]
    halves = [
        jnp.dot(taps, (spread == at * ch).astype(taps.dtype), preferred_element_type=jnp.float32).astype(taps.dtype)
        for at in range(2)
    ]
    for v in range(3):
        left, right = (h[3 * v * ch : 3 * (v + 1) * ch] for h in halves)
        base = 4 * v * ch
        banded[base : base + ch] = left[0:ch]
        banded[base + ch : base + 3 * ch] = left[ch:] + right[: 2 * ch]
        banded[base + 3 * ch : base + 4 * ch] = right[2 * ch :]

    for t in range(count):

        @pl.when(tissue(t) == 1)
        def _():
            fetch(t).wait()

    total = sum(tissue(t) for t in range(count))

    def store(t, at):
        return pltpu.make_async_copy(made.at[at], tiles.at[at], out_sem.at[t])

    def hand_on(t, at):
        return pltpu.make_async_copy(made.at[at], tail.at[at - (total - SHIFT_MOST)], tail_sem.at[t])

    def each(t, at):
        live = tissue(t) == 1

        @pl.when(live)
        def _():
            row, col = t // cols, t % cols
            window = band[
                pl.ds(pl.multiple_of(row * side, GUARD), side + 2 * GUARD),
                pl.ds(pl.multiple_of(col * wide, LANES), wide + 2 * LANES),
            ].astype(jnp.float32)
            window = window[:, LANES // 2 : LANES // 2 + wide + LANES]
            for v in range(3):
                shifted[v] = window[GUARD + v - 1 : GUARD + v - 1 + side].astype(band.dtype)
            pairs = wide // LANES
            total_rows = None
            for v in range(3):
                left = jnp.concatenate([shifted[v, :, p * LANES : p * LANES + 2 * LANES] for p in range(pairs)], axis=0)
                part = jnp.dot(left, banded[4 * v * ch : 4 * (v + 1) * ch], preferred_element_type=jnp.float32)
                total_rows = part if total_rows is None else total_rows + part
            result = (total_rows + bias[...]).astype(band.dtype)
            for p in range(pairs):
                made[at, :, p * LANES : (p + 1) * LANES] = result[p * side : (p + 1) * side]
            store(t, at).start()

            @pl.when(at >= total - SHIFT_MOST)
            def _():
                hand_on(t, at).start()

        return at + tissue(t)

    lax.fori_loop(0, count, each, jnp.int32(0))

    def finish(t, at):
        @pl.when(tissue(t) == 1)
        def _():
            store(t, at).wait()

            @pl.when(at >= total - SHIFT_MOST)
            def _():
                hand_on(t, at).wait()

        return at + tissue(t)

    lax.fori_loop(0, count, finish, jnp.int32(0))


def convolve(mask, pixels, above, below, weight, bias):
    rows, cols = mask.shape
    side = pixels.shape[0] // rows
    ch = weight.shape[2]
    wide = side * ch
    most = SLOTS + SHIFT_MOST
    dtype = pixels.dtype
    smem = pl.BlockSpec(memory_space=pltpu.SMEM)
    vmem = pl.BlockSpec(memory_space=pltpu.VMEM)
    hbm = pl.BlockSpec(memory_space=pl.ANY)
    return pl.pallas_call(
        functools.partial(conv_kernel, rows=rows, cols=cols, side=side, ch=ch),
        in_specs=[smem, hbm, vmem, vmem, vmem, vmem],
        out_specs=[hbm, hbm],
        out_shape=[
            jax.ShapeDtypeStruct((most, side, wide), dtype),
            jax.ShapeDtypeStruct((SHIFT_MOST, side, wide), dtype),
        ],
        scratch_shapes=[
            pltpu.VMEM((rows * side + 2 * GUARD, cols * wide + 2 * LANES), dtype),
            pltpu.VMEM((3, side, wide + LANES), dtype),
            pltpu.VMEM((12 * ch, 2 * ch), dtype),
            pltpu.VMEM((most, side, wide), dtype),
            pltpu.SemaphoreType.DMA((rows * cols,)),
            pltpu.SemaphoreType.DMA((rows * cols,)),
            pltpu.SemaphoreType.DMA((rows * cols,)),
        ],
    )(
        mask,
        pixels,
        above,
        below,
        weight.reshape(9 * ch, ch),
        jnp.tile(bias.astype(jnp.float32), 2).reshape(1, 2 * ch),
    )


def place_kernel(excess, own, passed, out, sem):
    shift = excess[0]

    def copy_own(i):
        return pltpu.make_async_copy(own.at[i - shift], out.at[i], sem.at[i])

    def copy_passed(i):
        return pltpu.make_async_copy(passed.at[i + SHIFT_MOST - shift], out.at[i], sem.at[i])

    for act in ("start", "wait"):
        for i in range(out.shape[0]):
            if i < SHIFT_MOST:

                @pl.when(i < shift)
                def _():
                    getattr(copy_passed(i), act)()

                @pl.when(i >= shift)
                def _():
                    getattr(copy_own(i), act)()

            else:
                getattr(copy_own(i), act)()


def place(excess, own, passed):
    hbm = pl.BlockSpec(memory_space=pl.ANY)
    return pl.pallas_call(
        place_kernel,
        in_specs=[pl.BlockSpec(memory_space=pltpu.SMEM), hbm, hbm],
        out_specs=hbm,
        out_shape=jax.ShapeDtypeStruct((SLOTS,) + own.shape[1:], own.dtype),
        scratch_shapes=[pltpu.SemaphoreType.DMA((SLOTS,))],
    )(excess, own, passed)


def on_device(slide_pixels, tissue_mask, conv_weight, conv_bias):
    size = lax.axis_size("row")
    device = lax.axis_index("row")
    count = jnp.broadcast_to(jnp.sum(tissue_mask), (size, LANES))
    table = lax.all_to_all(count, "row", 0, 0, tiled=True)
    up = [(i, i + 1) for i in range(size - 1)]
    down = [(j, i) for i, j in up]
    first, last = edges(tissue_mask, slide_pixels)
    above = lax.ppermute(last, "row", up)
    below = lax.ppermute(first, "row", down)
    own, tail = convolve(tissue_mask, slide_pixels, above, below, conv_weight, conv_bias)
    passed = lax.ppermute(tail, "row", up)
    lower = jnp.arange(size, dtype=jnp.int32)[:, None] < device
    earlier = jnp.sum(jnp.where(lower, table, 0)[:, 0])
    excess = (earlier - device * SLOTS).astype(jnp.int32).reshape(1)
    return place(excess, own, passed)


def solution(mesh):
    spread = ("slides", "row")
    return jax.shard_map(
        on_device,
        mesh=mesh,
        in_specs=(P(spread, None), P(spread, None), P(), P()),
        out_specs=P(spread, None, None),
        check_vma=False,
    )
```

time: 157 us -> 98 us (0.62); the launches traced: 155 us -> 97.7 us
  local copies, waits for them, and re-layouts: 67.5 us -> 3.24 us
  Pallas kernels: 0 us -> 43 us
  blocking collectives: 25.7 us -> 0 us
  other arithmetic: 20.9 us -> 2.06 us
  starting transfers between devices: 27.8 us -> 40.4 us
  matrix products: 7.52 us -> 0 us
  waiting for transfers between devices: 4.62 us -> 8.26 us
    pallas_call x0 -> x3, Pallas kernels: none -> 43 us  [the longest x1 32.9 us: place(): pl.pallas_call(place_kernel, in_specs=[pl.BlockSpec(memory_space=pltpu.SM...]
    all_to_all x0 -> x1, starting transfers between devices: none -> 30.7 us  [on_device(): table = lax.all_to_all(count, 'row', 0, 0, tiled=True)]
    unnamed x2 -> x0, blocking collectives: 25.7 us -> none
    unnamed x39 -> x8, local copies, waits for them, and re-layouts: 20.5 us -> 1.33 us
    ppermute x3, starting transfers between devices: 27.8 us -> 9.67 us  [the longest x1 5.66 us: on_device(): below = lax.ppermute(first, 'row', down)]
    another operation x17 -> x2, local copies, waits for them, and re-layouts: 13.3 us -> 0.62 us  [convolve(): jnp.tile(bias.astype(jnp.float32), 2).reshape(1, 2 * ch)]
    mul x2 -> x0, local copies, waits for them, and re-layouts: 8.98 us -> none  [on_device(): blocks * keeps]
    slice x6 -> x0, local copies, waits for them, and re-layouts: 8.44 us -> none  [the longest x3 5.25 us: on_device(): widened[tile_row * side:tile_row * side + side + 2, tile_col * side:tile_...]
  transfers between devices with their start and end apart: 3 -> 4, of which waited for: 1 -> 2; matrix products, arithmetic and copies ran while one was open for 14% -> 1% of each run, Pallas kernels for 0% -> 10%
where the time goes in v1:
time: 98 us; the launch traced here: 97.7 us
  Pallas kernels  43 us (44%)
  starting transfers between devices  40.4 us (41%)
  waiting for transfers between devices  8.26 us (8%)
  local copies, waits for them, and re-layouts  3.24 us (3%)
  other arithmetic  2.06 us (2%)
    pallas_call x1, Pallas kernels, place(): pl.pallas_call(place_kernel, in_specs=[pl.BlockSpec(memory_space=pltpu.SM...  32.9 us
    all_to_all x1, starting transfers between devices, on_device(): table = lax.all_to_all(count, 'row', 0, 0, tiled=True)  30.7 us
    pallas_call x1, Pallas kernels, convolve(): pl.pallas_call(functools.partial(conv_kernel, rows=rows, cols=cols, side=...  8.15 us
    ppermute x1, waiting for transfers between devices, on_device(): passed = lax.ppermute(tail, 'row', up)  6.7 us
    ppermute x1, starting transfers between devices, on_device(): below = lax.ppermute(first, 'row', down)  5.66 us
    ppermute x1, starting transfers between devices, on_device(): above = lax.ppermute(last, 'row', up)  2.06 us
  transfers between devices with their start and end apart: 4, of which 2 were waited for; matrix products, arithmetic and copies ran while one was open for 1% of the time, Pallas kernels for 10%

profile of v1, /device:TPU:44, one launch (start us, length us, event | category | flops | bytes accessed | tf_op | source)
XLA Modules:
  0.0 97.7 jit_solution(12605861366279066363)
XLA Ops:
  0.0 1.3 %reduce_sum.18 = s32[]{:T(128)} reduce(s32[2,8]{1,0:T(2,128)} %mask.3, s32[]{:T(128)} %constant.1.clone.1), dimensions={0,1}, to_apply=%region_0.0 | reduce | flops 15 | bytes 72 | tf_op jit(solution)/shard_map/reduce_sum | solution.py:232
  1.3 1.3 %broadcast_in_dim.17 = s32[128,1,128]{2,1,0:T(1,128)} broadcast(s32[]{:T(128)} %reduce_sum.18), dimensions={} | broadcast | bytes 65540 | tf_op jit(solution)/shard_map/broadcast_in_dim | solution.py:232
  2.6 30.7 %all-to-all-start = ((s32[128,1,128]{2,1,0:T(1,128)}), s32[128,1,128]{2,1,0:T(1,128)S(1)}, u32[]{:S(2)}, u32[]{:S(2)}) async-start(s32[128,1,128]{2,1,0:T(1,128)} %broadcast_in_dim.17), calls=%async_computation | async-start | bytes 131072 | tf_op jit(solution)/shard_map/all_to_all | solution.py:233
  33.3 0.0 copy-start.3
  33.3 1.9 %shard_map.46 = (bf16[1,16384]{1,0:T(2,128)(2,1)}, bf16[1,16384]{1,0:T(2,128)(2,1)}) custom-call(s32[2,8]{1,0:T(2,128)} %mask.3, bf16[64,16384]{1,0:T(8,128)(2,1)} %pixels.1, bf16[64,16384]{1,0:T(8,128)(2,1)} %pixels.1), custom_call_target="tpu_custom_call" | custom-call | tf_op jit(solution)/shard_map/pallas_call | solution.py:31
  35.3 2.1 %collective-permute-start = (bf16[1,16384]{1,0:T(2,128)(2,1)}, bf16[1,16384]{1,0:T(2,128)(2,1)S(1)}, u32[]{:S(2)}, u32[]{:S(2)}) collective-permute-start(bf16[1,16384]{1,0:T(2,128)(2,1)} %get-tuple-element.9), channel_id=1, source_target_pairs={{0,1},{1,2},{2,3},{3,4},{4,5},{5,6},{6,7},{7,8},{8,9},{9,10},{10,1... | collective-permute-start | bytes 98312 | tf_op jit(solution)/shard_map/ppermute | solution.py:237
  37.3 5.7 %collective-permute-start.1 = (bf16[1,16384]{1,0:T(2,128)(2,1)}, bf16[1,16384]{1,0:T(2,128)(2,1)S(1)}, u32[]{:S(2)}, u32[]{:S(2)}) collective-permute-start(bf16[1,16384]{1,0:T(2,128)(2,1)} %get-tuple-element.10), channel_id=1, source_target_pairs={{1,0},{2,1},{3,2},{4,3},{5,4},{6,5},{7,6},{8,7},{9,8},{10,9},{11,1... | collective-permute-start | bytes 98312 | tf_op jit(solution)/shard_map/ppermute | solution.py:238
  43.0 0.0 copy-done.3
  43.0 0.6 reshape_tile.3.bias
  43.6 0.0 collective-permute-done.above
  43.6 0.0 copy-start.1
  43.6 1.6 %collective-permute-done.1.below = bf16[1,16384]{1,0:T(2,128)(2,1)S(1)} collective-permute-done((bf16[1,16384]{1,0:T(2,128)(2,1)}, bf16[1,16384]{1,0:T(2,128)(2,1)S(1)}, u32[]{:S(2)}, u32[]{:S(2)}) %collective-permute-start.1) | collective-permute-done | bytes 32800 | tf_op jit(solution)/shard_map/ppermute | solution.py:238
  45.2 0.0 copy-start.2
  45.2 0.0 copy-done.1
  45.2 0.6 copy-done.2
  45.8 8.2 %shard_map.47 = (bf16[10,32,2048]{2,1,0:T(8,128)(2,1)}, bf16[2,32,2048]{2,1,0:T(8,128)(2,1)}) custom-call(s32[2,8]{1,0:T(2,128)} %mask.3, bf16[64,16384]{1,0:T(8,128)(2,1)} %pixels.1, bf16[1,16384]{1,0:T(2,128)(2,1)} %copy-done.1, bf16[1,16384]{1,0:T(2,128)(2,1)} %copy-done.2, bf16[576,64]{1,0:T(8,128)(2,1)} %bitcast.4, f32[1,128]{1,0:T(1,128)} %reshape_tile.3.bias), custom_call_target="tpu_custom_call" | custom-call | tf_op jit(solution)/shard_map/pallas_call | solution.py:166
  54.0 2.0 %collective-permute-start.2 = (bf16[2,32,2048]{2,1,0:T(8,128)(2,1)}, bf16[2,32,2048]{2,1,0:T(8,128)(2,1)S(1)}, u32[]{:S(2)}, u32[]{:S(2)}) collective-permute-start(bf16[2,32,2048]{2,1,0:T(8,128)(2,1)} %get-tuple-element.12), channel_id=1, source_target_pairs={{0,1},{1,2},{2,3},{3,4},{4,5},{5,6},{6,7},{7,8},{8,9},{9,10},{10,1... | collective-permute-start | bytes 786440 | tf_op jit(solution)/shard_map/ppermute | solution.py:240
  56.0 0.0 all-to-all-done
  56.0 0.7 fusion
  57.3 6.7 %collective-permute-done.2.passed = bf16[2,32,2048]{2,1,0:T(8,128)(2,1)S(1)} collective-permute-done((bf16[2,32,2048]{2,1,0:T(8,128)(2,1)}, bf16[2,32,2048]{2,1,0:T(8,128)(2,1)S(1)}, u32[]{:S(2)}, u32[]{:S(2)}) %collective-permute-start.2) | collective-permute-done | bytes 262176 | tf_op jit(solution)/shard_map/ppermute | solution.py:240
  64.0 0.0 copy-start
  64.0 0.7 copy-done
  64.7 32.9 %shard_map.48 = bf16[8,32,2048]{2,1,0:T(8,128)(2,1)} custom-call(s32[1]{0:T(128)} %bitcast.1.excess, bf16[10,32,2048]{2,1,0:T(8,128)(2,1)} %get-tuple-element.11.own, bf16[2,32,2048]{2,1,0:T(8,128)(2,1)} %copy-done), custom_call_target="tpu_custom_call" | custom-call | tf_op jit(solution)/shard_map/pallas_call | solution.py:220
  (2 shorter events, 0.0 us)
Async XLA Ops:
  2.6 53.4 %all-to-all-start = ((s32[128,1,128]{2,1,0:T(1,128)}), s32[128,1,128]{2,1,0:T(1,128)S(1)}, u32[]{:S(2)}, u32[]{:S(2)}) async-start(s32[128,1,128]{2,1,0:T(1,128)} %broadcast_in_dim.17), calls=%async_computation | async-start | bytes 131072 | tf_op jit(solution)/shard_map/all_to_all | solution.py:233
  33.3 9.7 %copy-start.3 = (bf16[64]{0:T(256)(128)(2,1)S(1)}, bf16[64]{0:T(256)(128)(2,1)}, u32[]{:S(2)}) copy-start(bf16[64]{0:T(256)(128)(2,1)} %param.7) | copy-start | bytes 388
  35.3 8.4 %collective-permute-start = (bf16[1,16384]{1,0:T(2,128)(2,1)}, bf16[1,16384]{1,0:T(2,128)(2,1)S(1)}, u32[]{:S(2)}, u32[]{:S(2)}) collective-permute-start(bf16[1,16384]{1,0:T(2,128)(2,1)} %get-tuple-element.9), channel_id=1, source_target_pairs={{0,1},{1,2},{2,3},{3,4},{4,5},{5,6},{6,7},{7,8},{8,9},{9,10},{10,1... | collective-permute-start | bytes 98312 | tf_op jit(solution)/shard_map/ppermute | solution.py:237
  37.3 7.9 %collective-permute-start.1 = (bf16[1,16384]{1,0:T(2,128)(2,1)}, bf16[1,16384]{1,0:T(2,128)(2,1)S(1)}, u32[]{:S(2)}, u32[]{:S(2)}) collective-permute-start(bf16[1,16384]{1,0:T(2,128)(2,1)} %get-tuple-element.10), channel_id=1, source_target_pairs={{1,0},{2,1},{3,2},{4,3},{5,4},{6,5},{7,6},{8,7},{9,8},{10,9},{11,1... | collective-permute-start | bytes 98312 | tf_op jit(solution)/shard_map/ppermute | solution.py:238
  43.6 1.6 %copy-start.1 = (bf16[1,16384]{1,0:T(2,128)(2,1)}, bf16[1,16384]{1,0:T(2,128)(2,1)S(1)}, u32[]{:S(2)}) copy-start(bf16[1,16384]{1,0:T(2,128)(2,1)S(1)} %collective-permute-done.above) | copy-start | bytes 98308
  45.2 0.6 copy-start.2
  54.0 10.0 %collective-permute-start.2 = (bf16[2,32,2048]{2,1,0:T(8,128)(2,1)}, bf16[2,32,2048]{2,1,0:T(8,128)(2,1)S(1)}, u32[]{:S(2)}, u32[]{:S(2)}) collective-permute-start(bf16[2,32,2048]{2,1,0:T(8,128)(2,1)} %get-tuple-element.12), channel_id=1, source_target_pairs={{0,1},{1,2},{2,3},{3,4},{4,5},{5,6},{6,7},{7,8},{8,9},{9,10},{10,1... | collective-permute-start | bytes 786440 | tf_op jit(solution)/shard_map/ppermute | solution.py:240
  64.0 0.7 copy-start

commit v2 on v1

v2 whole, which is shorter than its diff:
```python
import functools

import jax
import jax.numpy as jnp
from jax import lax
from jax.experimental import pallas as pl
from jax.experimental.pallas import tpu as pltpu
from jax.sharding import PartitionSpec as P

SLOTS = 8
SHIFT_MOST = 2
LANES = 128
GUARD = 16
RIM = 8


def fetch_band(mask, pixels, band, sem, *, rows, cols, side, wide, guard):
    def fetch(t):
        row, col = t // cols, t % cols
        return pltpu.make_async_copy(
            pixels.at[pl.ds(row * side, side), pl.ds(col * wide, wide)],
            band.at[pl.ds(guard + row * side, side), pl.ds(LANES + col * wide, wide)],
            sem.at[t],
        )

    for t in range(rows * cols):
        row, col = t // cols, t % cols

        @pl.when(mask[row, col] == 1)
        def _():
            fetch(t).start()

    for t in range(rows * cols):
        row, col = t // cols, t % cols

        @pl.when(mask[row, col] != 1)
        def _():
            band[guard + row * side : guard + (row + 1) * side, LANES + col * wide : LANES + (col + 1) * wide] = (
                jnp.zeros((side, wide), band.dtype)
            )

    edge = jnp.zeros((band.shape[0], LANES), band.dtype)
    band[:, 0:LANES] = edge
    band[:, LANES + cols * wide :] = edge

    def wait():
        for t in range(rows * cols):

            @pl.when(mask[t // cols, t % cols] == 1)
            def _():
                fetch(t).wait()

    return wait


def prepare_kernel(mask, pixels, card, first, last, parcel, band, sem, *, rows, cols, side, wide):
    count = rows * cols
    wait = fetch_band(mask, pixels, band, sem, rows=rows, cols=cols, side=side, wide=wide, guard=0)
    total = jnp.int32(0)
    for t in range(count):
        total = total + mask[t // cols, t % cols]
    places = []
    for k in range(SHIFT_MOST):
        rank, found = jnp.int32(0), jnp.int32(0)
        for t in range(count):
            hit = (mask[t // cols, t % cols] == 1) & (rank == total - SHIFT_MOST + k)
            found = jnp.where(hit, t, found)
            rank = rank + mask[t // cols, t % cols]
        places.append((found // cols, found % cols))
    lane = lax.broadcasted_iota(jnp.int32, card.shape, 2)
    info = jnp.where(lane == 0, total, 0)
    for k, (row, col) in enumerate(places):
        info = jnp.where(lane == 1 + 2 * k, row, jnp.where(lane == 2 + 2 * k, col, info))
    card[...] = info
    wait()
    first[...] = band[0:1, LANES : LANES + cols * wide]
    last[...] = band[rows * side - 1 :, LANES : LANES + cols * wide]
    window = wide + 2 * LANES
    line = lax.broadcasted_iota(jnp.int32, (RIM, window), 0)
    per = cols // SHIFT_MOST
    for k, (row, col) in enumerate(places):
        lanes = pl.ds(pl.multiple_of(col * wide, LANES), window)
        parcel[k, 0:side] = band[pl.ds(pl.multiple_of(row * side, side), side), lanes]
        near = band[pl.ds(pl.multiple_of(side - GUARD * row, GUARD), GUARD), lanes].astype(jnp.float32)
        rim = jnp.where(row == 0, near[0:1], near[GUARD - 1 : GUARD])
        block = jnp.broadcast_to(rim, (RIM, window))
        for j in range(per):
            at = (k * per + j) * wide
            low = band[rows * side - GUARD :, at : at + window].astype(jnp.float32)[GUARD - 1 : GUARD]
            block = jnp.where(line == 1 + j, jnp.broadcast_to(low, (RIM, window)), block)
        parcel[k, side:] = block.astype(parcel.dtype)


def prepare(mask, pixels, size):
    rows, cols = mask.shape
    side = pixels.shape[0] // rows
    wide = pixels.shape[1] // cols
    dtype = pixels.dtype
    vmem = pl.BlockSpec(memory_space=pltpu.VMEM)
    return pl.pallas_call(
        functools.partial(prepare_kernel, rows=rows, cols=cols, side=side, wide=wide),
        in_specs=[pl.BlockSpec(memory_space=pltpu.SMEM), pl.BlockSpec(memory_space=pl.ANY)],
        out_specs=[vmem, vmem, vmem, vmem],
        out_shape=[
            jax.ShapeDtypeStruct((size, 1, LANES), jnp.int32),
            jax.ShapeDtypeStruct((1, cols * wide), dtype),
            jax.ShapeDtypeStruct((1, cols * wide), dtype),
            jax.ShapeDtypeStruct((SHIFT_MOST, side + RIM, wide + 2 * LANES), dtype),
        ],
        scratch_shapes=[
            pltpu.VMEM((rows * side, cols * wide + 2 * LANES), dtype),
            pltpu.SemaphoreType.DMA((rows * cols,)),
        ],
    )(mask, pixels)


def conv_kernel(
    info, mask, pixels, parcel, farther, below, weight, bias, out,
    band, beyond, moved, shifted, banded, made, in_sem, out_sem,
    *, rows, cols, side, ch,
):
    wide = side * ch
    count = rows * cols
    window = wide + 2 * LANES
    slots = out.shape[0]
    excess = info[0]
    wait = fetch_band(mask, pixels, band, in_sem, rows=rows, cols=cols, side=side, wide=wide, guard=GUARD)

    per = cols // SHIFT_MOST
    for col in range(cols):
        row = parcel[col // per, side : side + RIM, LANES : LANES + wide].astype(jnp.float32)
        row = row[1 + col % per : 2 + col % per]
        at = LANES + col * wide
        band[0:GUARD, at : at + wide] = jnp.broadcast_to(row, (GUARD, wide)).astype(band.dtype)
    inner = pl.ds(LANES, cols * wide)
    band[GUARD + rows * side :, inner] = jnp.broadcast_to(below[...], (GUARD, cols * wide))
    beyond[:, inner] = jnp.broadcast_to(farther[...], (GUARD, cols * wide))
    edge = jnp.zeros((GUARD, LANES), band.dtype)
    beyond[:, 0:LANES] = edge
    beyond[:, LANES + cols * wide :] = edge

    spread = lax.broadcasted_iota(jnp.int32, (ch, 2 * ch), 1) - lax.broadcasted_iota(jnp.int32, (ch, 2 * ch), 0)
    taps = weight[...]
    halves = [
        jnp.dot(taps, (spread == at * ch).astype(taps.dtype), preferred_element_type=jnp.float32).astype(taps.dtype)
        for at in range(2)
    ]
    for v in range(3):
        left, right = (h[3 * v * ch : 3 * (v + 1) * ch] for h in halves)
        base = 4 * v * ch
        banded[base : base + ch] = left[0:ch]
        banded[base + ch : base + 3 * ch] = left[ch:] + right[: 2 * ch]
        banded[base + 3 * ch : base + 4 * ch] = right[2 * ch :]

    wait()

    for k in range(SHIFT_MOST):
        row, col = info[1 + 2 * k], info[2 + 2 * k]
        lanes = pl.ds(pl.multiple_of(col * wide, LANES), window)
        moved[k, GUARD : GUARD + side] = parcel[k, 0:side]
        rim = parcel[k, side : side + RIM].astype(jnp.float32)[0:1]
        rim = jnp.broadcast_to(rim, (GUARD, window)).astype(band.dtype)

        @pl.when(row == 0)
        def _():
            moved[k, 0:GUARD] = beyond[:, lanes]
            moved[k, GUARD + side :] = rim

        @pl.when(row != 0)
        def _():
            moved[k, 0:GUARD] = rim
            moved[k, GUARD + side :] = band[GUARD : 2 * GUARD, lanes]

    blocks = wide // LANES + 1

    def emit(source, slot):
        tile = source[:, LANES // 2 : LANES // 2 + blocks * LANES].astype(jnp.float32)
        for q in range(blocks):
            shifted[q] = tile[GUARD - RIM : GUARD + side + RIM, q * LANES : (q + 1) * LANES]
        result = None
        for v in range(3):
            start = RIM + v - 1
            part = [shifted[q, start : start + side].astype(band.dtype) for q in range(blocks)]
            left = jnp.concatenate(
                [jnp.concatenate([part[q], part[q + 1]], axis=1) for q in range(blocks - 1)], axis=0
            )
            term = jnp.dot(left, banded[4 * v * ch : 4 * (v + 1) * ch], preferred_element_type=jnp.float32)
            result = term if result is None else result + term
        result = (result + bias[...]).astype(band.dtype)
        for q in range(blocks - 1):
            made[slot, :, q * LANES : (q + 1) * LANES] = result[q * side : (q + 1) * side]
        pltpu.make_async_copy(made.at[slot], out.at[slot], out_sem.at[slot]).start()

    def own(t, rank):
        row, col = t // cols, t % cols
        slot = rank + excess

        @pl.when((mask[row, col] == 1) & (slot < slots))
        def _():
            emit(
                band[
                    pl.ds(pl.multiple_of(row * side, GUARD), side + 2 * GUARD),
                    pl.ds(pl.multiple_of(col * wide, LANES), window),
                ],
                slot,
            )

        return rank + mask[row, col]

    lax.fori_loop(0, count, own, jnp.int32(0))

    def taken(k, carry):
        slot = k + excess - SHIFT_MOST

        @pl.when(slot >= 0)
        def _():
            emit(moved[k], slot)

        return carry

    lax.fori_loop(0, SHIFT_MOST, taken, jnp.int32(0))

    for slot in range(slots):
        pltpu.make_async_copy(made.at[slot], out.at[slot], out_sem.at[slot]).wait()


def convolve(info, mask, pixels, parcel, farther, below, weight, bias):
    rows, cols = mask.shape
    side = pixels.shape[0] // rows
    ch = weight.shape[2]
    wide = side * ch
    dtype = pixels.dtype
    smem = pl.BlockSpec(memory_space=pltpu.SMEM)
    vmem = pl.BlockSpec(memory_space=pltpu.VMEM)
    hbm = pl.BlockSpec(memory_space=pl.ANY)
    return pl.pallas_call(
        functools.partial(conv_kernel, rows=rows, cols=cols, side=side, ch=ch),
        in_specs=[smem, smem, hbm, vmem, vmem, vmem, vmem, vmem],
        out_specs=hbm,
        out_shape=jax.ShapeDtypeStruct((SLOTS, side, wide), dtype),
        scratch_shapes=[
            pltpu.VMEM((rows * side + 2 * GUARD, cols * wide + 2 * LANES), dtype),
            pltpu.VMEM((GUARD, cols * wide + 2 * LANES), dtype),
            pltpu.VMEM((SHIFT_MOST, side + 2 * GUARD, wide + 2 * LANES), dtype),
            pltpu.VMEM((wide // LANES + 1, side + 2 * RIM, LANES), jnp.float32),
            pltpu.VMEM((12 * ch, 2 * ch), dtype),
            pltpu.VMEM((SLOTS, side, wide), dtype),
            pltpu.SemaphoreType.DMA((rows * cols,)),
            pltpu.SemaphoreType.DMA((SLOTS,)),
        ],
    )(
        info,
        mask,
        pixels,
        parcel,
        farther,
        below,
        weight.reshape(9 * ch, ch),
        jnp.tile(bias.astype(jnp.float32), 2).reshape(1, 2 * ch),
    )


def on_device(slide_pixels, tissue_mask, conv_weight, conv_bias):
    size = lax.axis_size("row")
    device = lax.axis_index("row")
    card, first, last, parcel = prepare(tissue_mask, slide_pixels, size)
    table = lax.all_to_all(card, "row", 0, 0, tiled=True)
    up = [(i, i + 1) for i in range(size - 1)]
    up_two = [(i, i + 2) for i in range(size - 2)]
    down = [(i + 1, i) for i in range(size - 1)]
    parcel = lax.ppermute(parcel, "row", up)
    below = lax.ppermute(first, "row", down)
    farther = lax.ppermute(last, "row", up_two)
    sender = jnp.arange(size, dtype=jnp.int32)[:, None]
    lane = jnp.arange(LANES, dtype=jnp.int32)[None, :]
    wanted = jnp.where(lane == 0, sender < device, sender == device - 1)
    info = jnp.sum(jnp.where(wanted, table.reshape(size, LANES), 0), axis=0)
    info = info - jnp.where(lane[0] == 0, device * SLOTS, 0).astype(jnp.int32)
    return convolve(info, tissue_mask, slide_pixels, parcel, farther, below, conv_weight, conv_bias)


def solution(mesh):
    spread = ("slides", "row")
    return jax.shard_map(
        on_device,
        mesh=mesh,
        in_specs=(P(spread, None), P(spread, None), P(), P()),
        out_specs=P(spread, None, None),
        check_vma=False,
    )
```

time: 98 us -> 61.1 us (0.62)
  Pallas kernels: 43 us -> 10.2 us
  local copies, waits for them, and re-layouts: 3.24 us -> 1.35 us
  other arithmetic: 2.06 us -> 0.7 us
    pallas_call x2 -> x1, Pallas kernels: 34.9 us -> 3.22 us  [prepare(): pl.pallas_call(functools.partial(prepare_kernel, rows=rows, cols=cols, si...]
    all_to_all x1, waiting for transfers between devices: 0.01 us -> 3.24 us  [on_device(): table = lax.all_to_all(card, 'row', 0, 0, tiled=True)]
    ppermute x2, waiting for transfers between devices: 6.7 us -> 4.62 us  [the longest x1 4.62 us: on_device(): parcel = lax.ppermute(parcel, 'row', up)]
    reduce_sum x2 -> x1, other arithmetic: 2.05 us -> 0.11 us  [on_device(): info = jnp.sum(jnp.where(wanted, table.reshape(size, LANES), 0), axis=0)]
    ppermute x1, starting transfers between devices: 5.66 us -> 4.03 us  [on_device(): below = lax.ppermute(first, 'row', down)]
    ppermute x1, waiting for transfers between devices: 1.56 us -> 0.01 us  [on_device(): below = lax.ppermute(first, 'row', down)]
    ppermute x2, starting transfers between devices: 4.01 us -> 5.39 us  [the longest x1 3.44 us: on_device(): farther = lax.ppermute(last, 'row', up_two)]
    broadcast_in_dim x1 -> x0, local copies, waits for them, and re-layouts: 1.3 us -> none  [on_device(): count = jnp.broadcast_to(jnp.sum(tissue_mask), (size, LANES))]
  transfers between devices with their start and end apart: 4 -> 4, of which waited for: 2 -> 2; matrix products, arithmetic and copies ran while one was open for 1% -> 2% of each run, Pallas kernels for 10% -> 0%
where the time goes in v2:
time: 61.1 us; the launch traced here: 60.3 us
  starting transfers between devices  40.1 us (66%)
  Pallas kernels  10.2 us (17%)
  waiting for transfers between devices  7.86 us (13%)
  local copies, waits for them, and re-layouts  1.35 us (2%)
  other arithmetic  0.7 us (1%)
    all_to_all x1, starting transfers between devices, on_device(): table = lax.all_to_all(card, 'row', 0, 0, tiled=True)  30.6 us
    pallas_call x1, Pallas kernels, convolve(): pl.pallas_call(functools.partial(conv_kernel, rows=rows, cols=cols, side=...  7.01 us
    ppermute x1, waiting for transfers between devices, on_device(): parcel = lax.ppermute(parcel, 'row', up)  4.62 us
    ppermute x1, starting transfers between devices, on_device(): below = lax.ppermute(first, 'row', down)  4.03 us
    ppermute x1, starting transfers between devices, on_device(): farther = lax.ppermute(last, 'row', up_two)  3.44 us
    all_to_all x1, waiting for transfers between devices, on_device(): table = lax.all_to_all(card, 'row', 0, 0, tiled=True)  3.24 us
    pallas_call x1, Pallas kernels, prepare(): pl.pallas_call(functools.partial(prepare_kernel, rows=rows, cols=cols, si...  3.22 us
    ppermute x1, starting transfers between devices, on_device(): parcel = lax.ppermute(parcel, 'row', up)  1.95 us
  transfers between devices with their start and end apart: 4, of which 2 were waited for; matrix products, arithmetic and copies ran while one was open for 2% of the time, Pallas kernels for 0%

profile of v2, /device:TPU:44, one launch (start us, length us, event | category | flops | bytes accessed | tf_op | source)
XLA Modules:
  0.0 60.3 jit_solution(7583833949729782271)
XLA Ops:
  0.0 0.0 copy-start.3
  0.0 3.2 %shard_map.46 = (s32[128,1,128]{2,1,0:T(1,128)}, bf16[1,16384]{1,0:T(2,128)(2,1)}, bf16[1,16384]{1,0:T(2,128)(2,1)}, bf16[2,40,2304]{2,1,0:T(8,128)(2,1)}) custom-call(s32[2,8]{1,0:T(2,128)} %mask.3, bf16[64,16384]{1,0:T(8,128)(2,1)} %pixels.3), custom_call_target="tpu_custom_call" | custom-call | tf_op jit(solution)/shard_map/pallas_call | solution.py:100
  3.2 30.6 %all-to-all-start = ((s32[128,1,128]{2,1,0:T(1,128)}), s32[128,1,128]{2,1,0:T(1,128)S(1)}, u32[]{:S(2)}, u32[]{:S(2)}) async-start(s32[128,1,128]{2,1,0:T(1,128)} %get-tuple-element.9), calls=%async_computation | async-start | bytes 131072 | tf_op jit(solution)/shard_map/all_to_all | solution.py:267
  33.9 3.4 %collective-permute-start.1 = (bf16[1,16384]{1,0:T(2,128)(2,1)}, bf16[1,16384]{1,0:T(2,128)(2,1)S(1)}, u32[]{:S(2)}, u32[]{:S(2)}) collective-permute-start(bf16[1,16384]{1,0:T(2,128)(2,1)} %get-tuple-element.11), channel_id=1, source_target_pairs={{0,2},{1,3},{2,4},{3,5},{4,6},{5,7},{6,8},{7,9},{8,10},{9,11},{10,... | collective-permute-start | bytes 98312 | tf_op jit(solution)/shard_map/ppermute | solution.py:273
  37.3 4.0 %collective-permute-start.2 = (bf16[1,16384]{1,0:T(2,128)(2,1)}, bf16[1,16384]{1,0:T(2,128)(2,1)S(1)}, u32[]{:S(2)}, u32[]{:S(2)}) collective-permute-start(bf16[1,16384]{1,0:T(2,128)(2,1)} %get-tuple-element.12), channel_id=1, source_target_pairs={{1,0},{2,1},{3,2},{4,3},{5,4},{6,5},{7,6},{8,7},{9,8},{10,9},{11,1... | collective-permute-start | bytes 98312 | tf_op jit(solution)/shard_map/ppermute | solution.py:272
  41.4 2.0 %collective-permute-start = (bf16[2,40,2304]{2,1,0:T(8,128)(2,1)}, bf16[2,40,2304]{2,1,0:T(8,128)(2,1)S(1)}, u32[]{:S(2)}, u32[]{:S(2)}) collective-permute-start(bf16[2,40,2304]{2,1,0:T(8,128)(2,1)} %get-tuple-element.10), channel_id=1, source_target_pairs={{0,1},{1,2},{2,3},{3,4},{4,5},{5,6},{6,7},{7,8},{8,9},{9,10},{10,1... | collective-permute-start | bytes 1105928 | tf_op jit(solution)/shard_map/ppermute | solution.py:271
  43.4 0.0 copy-done.3
  43.4 0.6 reshape_tile.3.bias
  44.0 3.2 %all-to-all-done = s32[128,1,128]{2,1,0:T(1,128)S(1)} async-done(((s32[128,1,128]{2,1,0:T(1,128)}), s32[128,1,128]{2,1,0:T(1,128)S(1)}, u32[]{:S(2)}, u32[]{:S(2)}) %all-to-all-start) | async-done | bytes 65568 | tf_op jit(solution)/shard_map/all_to_all | solution.py:267
  47.2 0.1 select_reduce_fusion
  47.3 0.6 select_subtract_fusion.info
  47.9 0.0 collective-permute-done.1.farther
  47.9 0.0 copy-start.1
  47.9 0.0 collective-permute-done.2.below
  47.9 0.0 copy-start.2
  47.9 4.6 %collective-permute-done.parcel = bf16[2,40,2304]{2,1,0:T(8,128)(2,1)S(1)} collective-permute-done((bf16[2,40,2304]{2,1,0:T(8,128)(2,1)}, bf16[2,40,2304]{2,1,0:T(8,128)(2,1)S(1)}, u32[]{:S(2)}, u32[]{:S(2)}) %collective-permute-start) | collective-permute-done | bytes 368672 | tf_op jit(solution)/shard_map/ppermute | solution.py:271
  52.6 0.0 copy-start
  52.6 0.0 copy-done.1
  52.6 0.0 copy-done.2
  52.6 0.7 %copy-done = bf16[2,40,2304]{2,1,0:T(8,128)(2,1)} copy-done((bf16[2,40,2304]{2,1,0:T(8,128)(2,1)}, bf16[2,40,2304]{2,1,0:T(8,128)(2,1)S(1)}, u32[]{:S(2)}) %copy-start) | copy-done | bytes 368664
  53.3 7.0 %shard_map.47 = bf16[8,32,2048]{2,1,0:T(8,128)(2,1)} custom-call(s32[128]{0:T(128)} %select_subtract_fusion.info, s32[2,8]{1,0:T(2,128)} %mask.3, bf16[64,16384]{1,0:T(8,128)(2,1)} %pixels.3, bf16[2,40,2304]{2,1,0:T(8,128)(2,1)} %copy-done, bf16[1,16384]{1,0:T(2,128)(2,1)} %copy-done.1, bf16[1,16384]{1,0:T(2,128)(2,1)} %copy-done.2, ...), custom_call_target="tpu_custom_call" | custom-call | tf_op jit(solution)/shard_map/pallas_call | solution.py:236
  (3 shorter events, 0.0 us)
Async XLA Ops:
  0.0 43.4 %copy-start.3 = (bf16[64]{0:T(256)(128)(2,1)S(1)}, bf16[64]{0:T(256)(128)(2,1)}, u32[]{:S(2)}) copy-start(bf16[64]{0:T(256)(128)(2,1)} %param.7) | copy-start | bytes 388
  3.2 44.0 %all-to-all-start = ((s32[128,1,128]{2,1,0:T(1,128)}), s32[128,1,128]{2,1,0:T(1,128)S(1)}, u32[]{:S(2)}, u32[]{:S(2)}) async-start(s32[128,1,128]{2,1,0:T(1,128)} %get-tuple-element.9), calls=%async_computation | async-start | bytes 131072 | tf_op jit(solution)/shard_map/all_to_all | solution.py:267
  33.9 14.0 %collective-permute-start.1 = (bf16[1,16384]{1,0:T(2,128)(2,1)}, bf16[1,16384]{1,0:T(2,128)(2,1)S(1)}, u32[]{:S(2)}, u32[]{:S(2)}) collective-permute-start(bf16[1,16384]{1,0:T(2,128)(2,1)} %get-tuple-element.11), channel_id=1, source_target_pairs={{0,2},{1,3},{2,4},{3,5},{4,6},{5,7},{6,8},{7,9},{8,10},{9,11},{10,... | collective-permute-start | bytes 98312 | tf_op jit(solution)/shard_map/ppermute | solution.py:273
  37.3 10.6 %collective-permute-start.2 = (bf16[1,16384]{1,0:T(2,128)(2,1)}, bf16[1,16384]{1,0:T(2,128)(2,1)S(1)}, u32[]{:S(2)}, u32[]{:S(2)}) collective-permute-start(bf16[1,16384]{1,0:T(2,128)(2,1)} %get-tuple-element.12), channel_id=1, source_target_pairs={{1,0},{2,1},{3,2},{4,3},{5,4},{6,5},{7,6},{8,7},{9,8},{10,9},{11,1... | collective-permute-start | bytes 98312 | tf_op jit(solution)/shard_map/ppermute | solution.py:272
  41.4 11.2 %collective-permute-start = (bf16[2,40,2304]{2,1,0:T(8,128)(2,1)}, bf16[2,40,2304]{2,1,0:T(8,128)(2,1)S(1)}, u32[]{:S(2)}, u32[]{:S(2)}) collective-permute-start(bf16[2,40,2304]{2,1,0:T(8,128)(2,1)} %get-tuple-element.10), channel_id=1, source_target_pairs={{0,1},{1,2},{2,3},{3,4},{4,5},{5,6},{6,7},{7,8},{8,9},{9,10},{10,1... | collective-permute-start | bytes 1105928 | tf_op jit(solution)/shard_map/ppermute | solution.py:271
  47.9 4.6 %copy-start.1 = (bf16[1,16384]{1,0:T(2,128)(2,1)}, bf16[1,16384]{1,0:T(2,128)(2,1)S(1)}, u32[]{:S(2)}) copy-start(bf16[1,16384]{1,0:T(2,128)(2,1)S(1)} %collective-permute-done.1.farther) | copy-start | bytes 98308
  47.9 4.6 %copy-start.2 = (bf16[1,16384]{1,0:T(2,128)(2,1)}, bf16[1,16384]{1,0:T(2,128)(2,1)S(1)}, u32[]{:S(2)}) copy-start(bf16[1,16384]{1,0:T(2,128)(2,1)S(1)} %collective-permute-done.2.below) | copy-start | bytes 98308
  52.6 0.7 %copy-start = (bf16[2,40,2304]{2,1,0:T(8,128)(2,1)}, bf16[2,40,2304]{2,1,0:T(8,128)(2,1)S(1)}, u32[]{:S(2)}) copy-start(bf16[2,40,2304]{2,1,0:T(8,128)(2,1)S(1)} %collective-permute-done.parcel) | copy-start | bytes 1105924

commit v3 on v2

v3 whole, which is shorter than its diff:
```python
import functools

import jax
import jax.numpy as jnp
from jax import lax
from jax.experimental import pallas as pl
from jax.experimental.pallas import tpu as pltpu
from jax.sharding import PartitionSpec as P


SLOTS = 8
SHIFT_MOST = 2
LANES = 128
GUARD = 16
RIM = 8
ROOM = pltpu.CompilerParams(vmem_limit_bytes=16 * 2**20)


def fetch_band(mask, pixels, band, sem, *, rows, cols, side, wide, guard):
    def fetch(t):
        row, col = t // cols, t % cols
        return pltpu.make_async_copy(
            pixels.at[pl.ds(row * side, side), pl.ds(col * wide, wide)],
            band.at[pl.ds(guard + row * side, side), pl.ds(LANES + col * wide, wide)],
            sem.at[t],
        )

    for t in range(rows * cols):
        row, col = t // cols, t % cols

        @pl.when(mask[row, col] == 1)
        def _():
            fetch(t).start()

    for t in range(rows * cols):
        row, col = t // cols, t % cols

        @pl.when(mask[row, col] != 1)
        def _():
            band[guard + row * side : guard + (row + 1) * side, LANES + col * wide : LANES + (col + 1) * wide] = (
                jnp.zeros((side, wide), band.dtype)
            )

    edge = jnp.zeros((band.shape[0], LANES), band.dtype)
    band[:, 0:LANES] = edge
    band[:, LANES + cols * wide :] = edge

    def wait():
        for t in range(rows * cols):

            @pl.when(mask[t // cols, t % cols] == 1)
            def _():
                fetch(t).wait()

    return wait


def prepare_kernel(mask, pixels, card, first, last, parcel, band, sem, *, rows, cols, side, wide):
    count = rows * cols
    wait = fetch_band(mask, pixels, band, sem, rows=rows, cols=cols, side=side, wide=wide, guard=0)
    total = jnp.int32(0)
    for t in range(count):
        total = total + mask[t // cols, t % cols]
    places = []
    for k in range(SHIFT_MOST):
        rank, found = jnp.int32(0), jnp.int32(0)
        for t in range(count):
            hit = (mask[t // cols, t % cols] == 1) & (rank == total - SHIFT_MOST + k)
            found = jnp.where(hit, t, found)
            rank = rank + mask[t // cols, t % cols]
        places.append((found // cols, found % cols))
    lane = lax.broadcasted_iota(jnp.int32, card.shape, 2)
    info = jnp.where(lane == 0, total, 0)
    for k, (row, col) in enumerate(places):
        info = jnp.where(lane == 1 + 2 * k, row, jnp.where(lane == 2 + 2 * k, col, info))
    card[...] = info
    wait()
    first[...] = band[0:1, LANES : LANES + cols * wide]
    last[...] = band[rows * side - 1 :, LANES : LANES + cols * wide]
    window = wide + 2 * LANES
    line = lax.broadcasted_iota(jnp.int32, (RIM, window), 0)
    per = cols // SHIFT_MOST
    for k, (row, col) in enumerate(places):
        lanes = pl.ds(pl.multiple_of(col * wide, LANES), window)
        parcel[k, 0:side] = band[pl.ds(pl.multiple_of(row * side, side), side), lanes]
        near = band[pl.ds(pl.multiple_of(side - GUARD * row, GUARD), GUARD), lanes].astype(jnp.float32)
        rim = jnp.where(row == 0, near[0:1], near[GUARD - 1 : GUARD])
        block = jnp.broadcast_to(rim, (RIM, window))
        for j in range(per):
            at = (k * per + j) * wide
            low = band[rows * side - GUARD :, at : at + window].astype(jnp.float32)[GUARD - 1 : GUARD]
            block = jnp.where(line == 1 + j, jnp.broadcast_to(low, (RIM, window)), block)
        parcel[k, side:] = block.astype(parcel.dtype)


def prepare(mask, pixels, size):
    rows, cols = mask.shape
    side = pixels.shape[0] // rows
    wide = pixels.shape[1] // cols
    dtype = pixels.dtype
    vmem = pl.BlockSpec(memory_space=pltpu.VMEM)
    return pl.pallas_call(
        functools.partial(prepare_kernel, rows=rows, cols=cols, side=side, wide=wide),
        in_specs=[pl.BlockSpec(memory_space=pltpu.SMEM), pl.BlockSpec(memory_space=pl.ANY)],
        out_specs=[vmem] * 5,
        out_shape=[
            pltpu.VMEM((size, 1, LANES), jnp.int32),
            pltpu.VMEM((1, cols * wide), dtype),
            pltpu.VMEM((1, cols * wide), dtype),
            pltpu.VMEM((SHIFT_MOST, side + RIM, wide + 2 * LANES), dtype),
            pltpu.VMEM((rows * side, cols * wide + 2 * LANES), dtype),
        ],
        scratch_shapes=[pltpu.SemaphoreType.DMA((rows * cols,))],
        compiler_params=ROOM,
    )(pltpu.with_memory_space_constraint(mask, pltpu.HBM), pltpu.with_memory_space_constraint(pixels, pltpu.HBM))


def conv_kernel(
    device, table, mask, band, parcel, farther, below, weight, bias, out,
    over, under, beyond, moved, shifted, banded, made, out_sem,
    *, rows, cols, side, ch,
):
    wide = side * ch
    window = wide + 2 * LANES
    slots = out.shape[0]

    sender = lax.broadcasted_iota(jnp.int32, table.shape, 0)
    lane = lax.broadcasted_iota(jnp.int32, table.shape, 1)
    here = device[0]
    wanted = jnp.where(lane == 0, (sender < here).astype(jnp.int32), (sender == here - 1).astype(jnp.int32))
    facts = jnp.sum(table[...] * wanted, axis=0, keepdims=True)
    place = lax.broadcasted_iota(jnp.int32, facts.shape, 1)

    def fact(k):
        return jnp.sum(jnp.where(place == k, facts, 0))

    excess = fact(0) - here * slots

    inner = pl.ds(LANES, cols * wide)
    edge = jnp.zeros((GUARD, LANES), over.dtype)
    for rim in (over, under, beyond):
        rim[:, 0:LANES] = edge
        rim[:, LANES + cols * wide :] = edge
    per = cols // SHIFT_MOST
    for col in range(cols):
        row = parcel[col // per, side : side + RIM, LANES : LANES + wide].astype(jnp.float32)
        row = row[1 + col % per : 2 + col % per]
        at = LANES + col * wide
        over[:, at : at + wide] = jnp.broadcast_to(row, (GUARD, wide)).astype(over.dtype)
    under[:, inner] = jnp.broadcast_to(below[...], (GUARD, cols * wide))
    beyond[:, inner] = jnp.broadcast_to(farther[...], (GUARD, cols * wide))

    group = 2 * LANES // ch
    taps = weight[...]
    spread = lax.broadcasted_iota(jnp.int32, (ch, 2 * LANES), 1) - lax.broadcasted_iota(jnp.int32, (ch, 2 * LANES), 0)
    spots = [
        jnp.dot(taps, (spread == at * ch).astype(taps.dtype), preferred_element_type=jnp.float32).astype(taps.dtype)
        for at in range(group)
    ]
    for v in range(3):
        for i in range(group + 2):
            block = None
            for j in range(group):
                if 0 <= i - j <= 2:
                    tap = 3 * v + i - j
                    piece = spots[j][tap * ch : (tap + 1) * ch]
                    block = piece if block is None else block + piece
            at = (v * (group + 2) + i) * ch
            banded[at : at + ch] = block

    for k in range(SHIFT_MOST):
        row, col = fact(1 + 2 * k), fact(2 + 2 * k)
        lanes = pl.ds(pl.multiple_of(col * wide, LANES), window)
        moved[k, GUARD : GUARD + side] = parcel[k, 0:side]
        rim = parcel[k, side : side + RIM].astype(jnp.float32)[0:1]
        rim = jnp.broadcast_to(rim, (GUARD, window)).astype(moved.dtype)

        @pl.when(row == 0)
        def _():
            moved[k, 0:GUARD] = beyond[:, lanes]
            moved[k, GUARD + side :] = rim

        @pl.when(row != 0)
        def _():
            moved[k, 0:GUARD] = rim
            moved[k, GUARD + side :] = band[0:GUARD, lanes]

    blocks = wide // LANES + 1
    step = 2 * LANES

    def emit(top, middle, bottom, slot):
        inside = slice(LANES // 2, LANES // 2 + blocks * LANES)
        top = top[:, inside].astype(jnp.float32)[GUARD - RIM :]
        middle = middle[:, inside].astype(jnp.float32)
        bottom = bottom[:, inside].astype(jnp.float32)[:RIM]
        for q in range(blocks):
            lanes = slice(q * LANES, (q + 1) * LANES)
            shifted[q, 0:RIM] = top[:, lanes]
            shifted[q, RIM : RIM + side] = middle[:, lanes]
            shifted[q, RIM + side :] = bottom[:, lanes]
        parts = [
            [shifted[q, RIM + v - 1 : RIM + v - 1 + side].astype(out.dtype) for q in range(blocks)] for v in range(3)
        ]
        left = jnp.concatenate(
            [
                jnp.concatenate([parts[v][q + n] for v in range(3) for n in range(3)], axis=1)
                for q in range(0, blocks - 1, 2)
            ],
            axis=0,
        )
        result = jnp.dot(left, banded[...], preferred_element_type=jnp.float32)
        result = (result + bias[...]).astype(out.dtype)
        for g in range((blocks - 1) // 2):
            made[slot, :, g * step : (g + 1) * step] = result[g * side : (g + 1) * side]
        pltpu.make_async_copy(made.at[slot], out.at[slot], out_sem.at[slot]).start()

    rank = jnp.int32(0)
    for row in range(rows):

        def own(col, rank):
            slot = rank + excess

            @pl.when((mask[row, col] == 1) & (slot < slots))
            def _():
                lanes = pl.ds(pl.multiple_of(col * wide, LANES), window)
                top = over if row == 0 else band.at[row * side - GUARD : row * side]
                bottom = under if row == rows - 1 else band.at[(row + 1) * side : (row + 1) * side + GUARD]
                emit(top[:, lanes], band[row * side : (row + 1) * side, lanes], bottom[:, lanes], slot)

            return rank + mask[row, col]

        rank = lax.fori_loop(0, cols, own, rank)

    def taken(k, carry):
        slot = k + excess - SHIFT_MOST

        @pl.when(slot >= 0)
        def _():
            emit(moved[k, 0:GUARD], moved[k, GUARD : GUARD + side], moved[k, GUARD + side :], slot)

        return carry

    lax.fori_loop(0, SHIFT_MOST, taken, jnp.int32(0))

    for slot in range(slots):
        pltpu.make_async_copy(made.at[slot], out.at[slot], out_sem.at[slot]).wait()


def convolve(device, table, mask, band, parcel, farther, below, weight, bias):
    rows, cols = mask.shape
    side = band.shape[0] // rows
    ch = weight.shape[2]
    wide = side * ch
    dtype = band.dtype
    smem = pl.BlockSpec(memory_space=pltpu.SMEM)
    vmem = pl.BlockSpec(memory_space=pltpu.VMEM)
    hbm = pl.BlockSpec(memory_space=pl.ANY)
    rims = [pltpu.VMEM((GUARD, cols * wide + 2 * LANES), dtype)] * 3
    group = 2 * LANES // ch
    near = [
        table,
        band,
        parcel,
        farther,
        below,
        weight.reshape(9 * ch, ch),
        jnp.tile(bias.astype(jnp.float32), group).reshape(1, 2 * LANES),
    ]
    table, band, parcel, farther, below, weight, bias = (
        pltpu.with_memory_space_constraint(a, pltpu.VMEM) for a in near
    )
    return pl.pallas_call(
        functools.partial(conv_kernel, rows=rows, cols=cols, side=side, ch=ch),
        in_specs=[smem, vmem, smem, vmem, vmem, vmem, vmem, vmem, vmem],
        out_specs=hbm,
        out_shape=jax.ShapeDtypeStruct((SLOTS, side, wide), dtype),
        scratch_shapes=[
            *rims,
            pltpu.VMEM((SHIFT_MOST, side + 2 * GUARD, wide + 2 * LANES), dtype),
            pltpu.VMEM((wide // LANES + 1, side + 2 * RIM, LANES), jnp.float32),
            pltpu.VMEM((3 * (group + 2) * ch, 2 * LANES), dtype),
            pltpu.VMEM((SLOTS, side, wide), dtype),
            pltpu.SemaphoreType.DMA((SLOTS,)),
        ],
        compiler_params=ROOM,
    )(device, table, pltpu.with_memory_space_constraint(mask, pltpu.HBM), band, parcel, farther, below, weight, bias)


def on_device(slide_pixels, tissue_mask, conv_weight, conv_bias):
    size = lax.axis_size("row")
    device = lax.axis_index("row").astype(jnp.int32).reshape(1)
    card, first, last, parcel, band = prepare(tissue_mask, slide_pixels, size)
    up = [(i, i + 1) for i in range(size - 1)]
    up_two = [(i, i + 2) for i in range(size - 2)]
    down = [(i + 1, i) for i in range(size - 1)]
    parcel = lax.ppermute(parcel, "row", up)
    table = lax.all_to_all(card, "row", 0, 0, tiled=True)
    below = lax.ppermute(first, "row", down)
    farther = lax.ppermute(last, "row", up_two)
    table = table.reshape(size, LANES)
    return convolve(device, table, tissue_mask, band, parcel, farther, below, conv_weight, conv_bias)


def solution(mesh):
    spread = ("slides", "row")
    return jax.shard_map(
        on_device,
        mesh=mesh,
        in_specs=(P(spread, None), P(spread, None), P(), P()),
        out_specs=P(spread, None, None),
        check_vma=False,
    )
```

time: 61.1 us -> 58 us (0.949)
  the two profiles are of different devices: /device:TPU:44 before, /device:TPU:33 now
where the time goes in v3:
time: 58 us; the launch traced here: 57.8 us
  starting transfers between devices  40.2 us (69%)
  waiting for transfers between devices  8.93 us (15%)
  Pallas kernels  8.51 us (15%)
    all_to_all x1, starting transfers between devices, on_device(): table = lax.all_to_all(card, 'row', 0, 0, tiled=True)  28.4 us
    ppermute x1, starting transfers between devices, on_device(): parcel = lax.ppermute(parcel, 'row', up)  5.9 us
    all_to_all x1, waiting for transfers between devices, on_device(): table = lax.all_to_all(card, 'row', 0, 0, tiled=True)  5.68 us
    pallas_call x1, Pallas kernels, convolve(): pl.pallas_call(functools.partial(conv_kernel, rows=rows, cols=cols, side=...  5.59 us
    ppermute x1, starting transfers between devices, on_device(): farther = lax.ppermute(last, 'row', up_two)  3.29 us
    ppermute x1, waiting for transfers between devices, on_device(): below = lax.ppermute(first, 'row', down)  3.24 us
    pallas_call x1, Pallas kernels, prepare(): pl.pallas_call(functools.partial(prepare_kernel, rows=rows, cols=cols, si...  2.92 us
    ppermute x1, starting transfers between devices, on_device(): below = lax.ppermute(first, 'row', down)  2.61 us
  transfers between devices with their start and end apart: 4, of which 2 were waited for; matrix products, arithmetic and copies ran while one was open for 0% of the time, Pallas kernels for 0%

profile of v3, /device:TPU:33, one launch (start us, length us, event | category | flops | bytes accessed | tf_op | source)
XLA Modules:
  0.0 57.8 jit_solution(16367075861523283169)
XLA Ops:
  0.0 0.0 copy-start.1
  0.0 0.0 copy-start
  0.0 2.9 %shard_map.46 = (s32[128,1,128]{2,1,0:T(1,128)}, bf16[1,16384]{1,0:T(2,128)(2,1)S(1)}, bf16[1,16384]{1,0:T(2,128)(2,1)S(1)}, bf16[2,40,2304]{2,1,0:T(8,128)(2,1)S(1)}, bf16[64,16640]{1,0:T(8,128)(2,1)S(1)}) custom-call(s32[2,8]{1,0:T(2,128)} %mask.3, bf16[64,16384]{1,0:T(8,128)(2,1)} %pixels.1), custom_call_target="tpu_custom_call" | custom-call | tf_op jit(solution)/shard_map/pallas_call | solution.py:102
  2.9 5.9 %collective-permute-start = (bf16[2,40,2304]{2,1,0:T(8,128)(2,1)S(1)}, bf16[2,40,2304]{2,1,0:T(8,128)(2,1)S(1)}, u32[]{:S(2)}, u32[]{:S(2)}) collective-permute-start(bf16[2,40,2304]{2,1,0:T(8,128)(2,1)S(1)} %get-tuple-element.12), channel_id=1, source_target_pairs={{0,1},{1,2},{2,3},{3,4},{4,5},{5,6},{6,7},{7,8},{8,9},{9,10},{10,1... | collective-permute-start | bytes 1105928 | tf_op jit(solution)/shard_map/ppermute | solution.py:296
  8.8 28.4 %all-to-all-start = ((s32[128,1,128]{2,1,0:T(1,128)}), s32[128,1,128]{2,1,0:T(1,128)S(1)}, u32[]{:S(2)}, u32[]{:S(2)}) async-start(s32[128,1,128]{2,1,0:T(1,128)} %get-tuple-element.10), calls=%async_computation | async-start | bytes 131072 | tf_op jit(solution)/shard_map/all_to_all | solution.py:297
  37.2 3.3 %collective-permute-start.1 = (bf16[1,16384]{1,0:T(2,128)(2,1)S(1)}, bf16[1,16384]{1,0:T(2,128)(2,1)S(1)}, u32[]{:S(2)}, u32[]{:S(2)}) collective-permute-start(bf16[1,16384]{1,0:T(2,128)(2,1)S(1)} %get-tuple-element.13), channel_id=1, source_target_pairs={{0,2},{1,3},{2,4},{3,5},{4,6},{5,7},{6,8},{7,9},{8,10},{9,11},{10,... | collective-permute-start | bytes 98312 | tf_op jit(solution)/shard_map/ppermute | solution.py:299
  40.5 2.6 %collective-permute-start.2 = (bf16[1,16384]{1,0:T(2,128)(2,1)S(1)}, bf16[1,16384]{1,0:T(2,128)(2,1)S(1)}, u32[]{:S(2)}, u32[]{:S(2)}) collective-permute-start(bf16[1,16384]{1,0:T(2,128)(2,1)S(1)} %get-tuple-element.14), channel_id=1, source_target_pairs={{1,0},{2,1},{3,2},{4,3},{5,4},{6,5},{7,6},{8,7},{9,8},{10,9},{11,1... | collective-permute-start | bytes 98312 | tf_op jit(solution)/shard_map/ppermute | solution.py:298
  43.2 0.0 copy-done.1
  43.2 0.1 reshape_tile.3.bias
  43.3 0.0 collective-permute-done.1.farther
  43.3 3.2 %collective-permute-done.2.below = bf16[1,16384]{1,0:T(2,128)(2,1)S(1)} collective-permute-done((bf16[1,16384]{1,0:T(2,128)(2,1)S(1)}, bf16[1,16384]{1,0:T(2,128)(2,1)S(1)}, u32[]{:S(2)}, u32[]{:S(2)}) %collective-permute-start.2) | collective-permute-done | bytes 32800 | tf_op jit(solution)/shard_map/ppermute | solution.py:298
  46.5 5.7 %all-to-all-done = s32[128,1,128]{2,1,0:T(1,128)S(1)} async-done(((s32[128,1,128]{2,1,0:T(1,128)}), s32[128,1,128]{2,1,0:T(1,128)S(1)}, u32[]{:S(2)}, u32[]{:S(2)}) %all-to-all-start) | async-done | bytes 65568 | tf_op jit(solution)/shard_map/all_to_all | solution.py:297
  52.2 0.0 collective-permute-done.parcel
  52.2 0.0 copy-done
  52.2 5.6 %shard_map.47 = bf16[8,32,2048]{2,1,0:T(8,128)(2,1)} custom-call(s32[1]{0:T(128)} %bitcast.device, s32[128,128]{1,0:T(8,128)S(1)} %bitcast.3, s32[2,8]{1,0:T(2,128)} %mask.3, bf16[64,16640]{1,0:T(8,128)(2,1)S(1)} %get-tuple-element.11.band, bf16[2,40,2304]{2,1,0:T(8,128)(2,1)S(1)} %collective-permute-done.parcel, ...), custom_call_target="tpu_custom_call" | custom-call | tf_op jit(solution)/shard_map/pallas_call | solution.py:272
  (1 shorter events, 0.0 us)
Async XLA Ops:
  0.0 43.2 %copy-start.1 = (bf16[64]{0:T(256)(128)(2,1)S(1)}, bf16[64]{0:T(256)(128)(2,1)}, u32[]{:S(2)}) copy-start(bf16[64]{0:T(256)(128)(2,1)} %param.7) | copy-start | bytes 388
  0.0 52.2 %copy-start = (bf16[3,3,64,64]{3,2,1,0:T(8,128)(2,1)S(1)}, bf16[3,3,64,64]{3,2,1,0:T(8,128)(2,1)}, u32[]{:S(2)}) copy-start(bf16[3,3,64,64]{3,2,1,0:T(8,128)(2,1)} %param.6) | copy-start | bytes 221188
  2.9 49.3 %collective-permute-start = (bf16[2,40,2304]{2,1,0:T(8,128)(2,1)S(1)}, bf16[2,40,2304]{2,1,0:T(8,128)(2,1)S(1)}, u32[]{:S(2)}, u32[]{:S(2)}) collective-permute-start(bf16[2,40,2304]{2,1,0:T(8,128)(2,1)S(1)} %get-tuple-element.12), channel_id=1, source_target_pairs={{0,1},{1,2},{2,3},{3,4},{4,5},{5,6},{6,7},{7,8},{8,9},{9,10},{10,1... | collective-permute-start | bytes 1105928 | tf_op jit(solution)/shard_map/ppermute | solution.py:296
  8.8 43.4 %all-to-all-start = ((s32[128,1,128]{2,1,0:T(1,128)}), s32[128,1,128]{2,1,0:T(1,128)S(1)}, u32[]{:S(2)}, u32[]{:S(2)}) async-start(s32[128,1,128]{2,1,0:T(1,128)} %get-tuple-element.10), calls=%async_computation | async-start | bytes 131072 | tf_op jit(solution)/shard_map/all_to_all | solution.py:297
  37.2 6.0 %collective-permute-start.1 = (bf16[1,16384]{1,0:T(2,128)(2,1)S(1)}, bf16[1,16384]{1,0:T(2,128)(2,1)S(1)}, u32[]{:S(2)}, u32[]{:S(2)}) collective-permute-start(bf16[1,16384]{1,0:T(2,128)(2,1)S(1)} %get-tuple-element.13), channel_id=1, source_target_pairs={{0,2},{1,3},{2,4},{3,5},{4,6},{5,7},{6,8},{7,9},{8,10},{9,11},{10,... | collective-permute-start | bytes 98312 | tf_op jit(solution)/shard_map/ppermute | solution.py:299
  40.5 6.0 %collective-permute-start.2 = (bf16[1,16384]{1,0:T(2,128)(2,1)S(1)}, bf16[1,16384]{1,0:T(2,128)(2,1)S(1)}, u32[]{:S(2)}, u32[]{:S(2)}) collective-permute-start(bf16[1,16384]{1,0:T(2,128)(2,1)S(1)} %get-tuple-element.14), channel_id=1, source_target_pairs={{1,0},{2,1},{3,2},{4,3},{5,4},{6,5},{7,6},{8,7},{9,8},{10,9},{11,1... | collective-permute-start | bytes 98312 | tf_op jit(solution)/shard_map/ppermute | solution.py:298
